TPU v7x, 32 devices: a whole 2x2x4 slice. The times are simulated.
32 devices in a mesh: rep: 4 (over z), row: 2 (over x), col: 4 (over y, core).
Axes of the slice: x: 2, y: 2, z: 4, core: 2. Of those that a mesh axis runs over, the one named last changes fastest.
Arguments:
- grad_parts: bfloat16 [4, 8192, 8192], P('rep', 'row', 'col'), may hold values from -6 to 6
- momentum: float32 [8192, 8192], P(('row', 'rep'), 'col'), may hold values from -24 to 24
- basis: float32 [8192, 384], P('col'), may hold values from -0.0625 to 0.0625
Outputs:
- update: bfloat16 [8192, 8192], P('row', 'col')
- new_momentum: float32 [8192, 8192], P(('row', 'rep'), 'col')
- new_basis: float32 [8192, 384], P('col')
- power_norms: float32 [384], replicated
All inputs are finite; a program needn't handle non-finite values.
Results may differ from a plain program's by a relative error of at most 0.0085.
Values may be sent and summed in bfloat16 or wider, within the bound.
No kernel may reach another device: no remote copies, remote signals or barrier semaphores. Data moves between devices by JAX's collectives and lax.ppermute only.
A program may use at most 128 MiB of HBM per device.

v0:
```python
import jax
import jax.numpy as jnp
from jax import lax
from jax.sharding import PartitionSpec as P

D = 8192
RANK = 384
EPS = 1e-06
FEEDBACK = 0.05
HIGH = lax.Precision.HIGHEST


def local(grad_parts, momentum, basis):
    replicas = lax.axis_size("rep")
    local_grad = grad_parts[0].astype(jnp.float32)
    summed = lax.psum_scatter(
        local_grad.astype(jnp.bfloat16), "rep", scatter_dimension=0, tiled=True
    ).astype(jnp.float32)
    blended = momentum + summed / replicas
    power = jnp.dot(blended, basis, precision=HIGH)
    power = lax.psum(power, "col")
    squares = lax.psum(jnp.sum(power * power, axis=0), ("rep", "row"))
    power_norms = jnp.sqrt(squares / D)
    scaled = power / (jnp.sqrt(squares) + EPS)
    gram = lax.psum(jnp.dot(scaled.T, scaled, precision=HIGH), ("rep", "row"))
    factor = jnp.linalg.cholesky(gram)
    orth = jax.scipy.linalg.solve_triangular(factor, scaled.T, lower=True).T
    tile_orth = lax.all_gather(orth, "rep", axis=0, tiled=True)
    back = jnp.dot(blended.T, orth, precision=HIGH)
    back = lax.psum(back, ("rep", "row"))
    back_squares = lax.psum(jnp.sum(back * back, axis=0), "col")
    new_basis = back / (jnp.sqrt(back_squares) + EPS)
    new_momentum = blended - FEEDBACK * jnp.dot(orth, back.T, precision=HIGH)
    scale = D / RANK**0.5
    update = (scale * jnp.dot(tile_orth, new_basis.T, precision=HIGH)).astype(jnp.bfloat16)
    return (update, new_momentum, new_basis, power_norms)


def solution(mesh):
    placed = (P("rep", "row", "col"), P(("row", "rep"), "col"), P("col", None))
    return jax.shard_map(
        local,
        mesh=mesh,
        in_specs=placed,
        out_specs=(P("row", "col"), P(("row", "rep"), "col"), P("col", None), P()),
        check_vma=False,
    )
```

profile of v0, /device:TPU:0, one launch (start us, length us, event | category | flops | bytes accessed | tf_op | source)
XLA Modules:
  0.0 922.6 jit_solution(1023822813130225376)
XLA Ops:
  7.2 0.0 copy-start
  7.2 0.0 reduce-scatter.2.cloned.1.call-start
  7.2 0.7 reduce-scatter.2.cloned.1.call-update
  7.9 0.0 all-reduce.5.cloned.1.call-start
  8.0 285.6 %reduce-scatter.2.cloned.1.call-done = bf16[1024,2048]{1,0:T(8,128)(2,1)} async-done(((bf16[4096,2048]{1,0:T(8,128)(2,1)}), bf16[1024,2048]{1,0:T(8,128)(2,1)}) %reduce-scatter.2.cloned.1.call-update) | async-done | bytes 4194320 | tf_op jit(solution)/shard_map/reduce_scatter | solution.py:16
  293.5 17.7 %fusion.1 = f32[1024,384]{1,0:T(8,128)} fusion(f32[2048,384]{1,0:T(8,128)S(1)} %copy-done, f32[1024,2048]{1,0:T(8,128)} %param.4, bf16[1024,2048]{1,0:T(8,128)(2,1)} %reduce-scatter.2.cloned.1.call-done), kind=kOutput, calls=%fused_computation.7 | convolution fusion | flops 9669967872 | bytes 17301504 | tf_op jit(solution)/shard_map/dot_general | solution.py:20
  311.3 0.0 all-reduce.5.cloned.1.call-update
  311.3 0.0 all-reduce.7.cloned.1.call-start
  311.3 43.6 %all-reduce.5.cloned.1.call-done = f32[1024,384]{1,0:T(8,128)} async-done(((f32[1024,384]{1,0:T(8,128)}), f32[1024,384]{1,0:T(8,128)}) %all-reduce.5.cloned.1.call-update) | async-done | bytes 1572880 | tf_op jit(solution)/shard_map/psum | solution.py:21
  354.9 1.6 multiply_reduce_fusion.1
  356.5 21.4 %psum.36 = f32[384]{0:T(512)S(1)} all-reduce(f32[384]{0:T(512)S(1)} %multiply_reduce_fusion.1), channel_id=1, replica_groups=mesh['rep'=4,'row'=2,'col'=4] {'rep','row'}, use_global_device_ids=true, to_apply=%region_3.0 | all-reduce | flops 384 | bytes 3072 | tf_op jit(solution)/shard_map/psum | solution.py:22
  377.9 0.6 multiply_sqrt_fusion
  378.5 5.6 fusion.7
  384.0 0.0 all-reduce.7.cloned.1.call-update
  384.0 0.2 all-reduce.9.cloned.1.call-start
  384.3 0.1 fusion.6
  384.4 69.4 %all-reduce.7.cloned.1.call-done = f32[384,384]{0,1:T(8,128)} async-done(((f32[384,384]{0,1:T(8,128)}), f32[384,384]{0,1:T(8,128)}) %all-reduce.7.cloned.1.call-update) | async-done | bytes 589840 | tf_op jit(solution)/shard_map/psum | solution.py:25
  453.9 1.3 copy.8
  455.1 1.1 fusion.8
  456.3 11.7 %cholesky.77 = f32[128,128]{1,0:T(8,128)S(1)} custom-call(f32[128,128]{1,0:T(8,128)S(1)} %cholesky.192), custom_call_target="Cholesky" | custom-call | tf_op jit(solution)/shard_map/jit(cholesky)/cholesky | solution.py:26
  468.0 9.8 %custom-call.23 = f32[1,128,128]{1,2,0:T(8,128)S(1)} custom-call(f32[1,128,128]{2,1,0:T(8,128)S(1)} %get-tuple-element.28), custom_call_target="InvertDiagBlocksLowerTriangular" | custom-call | tf_op jit(solution)/shard_map/jit(cholesky)/cholesky | solution.py:26
  477.9 0.3 constant_dynamic-update-slice_fusion.2
  478.2 0.3 convolution_subtract_fusion.2
  478.5 11.7 %cholesky.162 = f32[128,128]{1,0:T(8,128)S(1)} custom-call(f32[128,128]{1,0:T(8,128)S(1)} %cholesky.196), custom_call_target="Cholesky" | custom-call | tf_op jit(solution)/shard_map/jit(cholesky)/cholesky | solution.py:26
  490.2 10.2 %custom-call.24 = f32[1,128,128]{1,2,0:T(8,128)S(1)} custom-call(f32[1,128,128]{2,1,0:T(8,128)S(1)} %get-tuple-element.25), custom_call_target="InvertDiagBlocksLowerTriangular" | custom-call | tf_op jit(solution)/shard_map/jit(cholesky)/cholesky | solution.py:26
  500.4 0.2 convolution_dynamic-update-slice_fusion
  500.6 0.3 convolution_subtract_fusion.3
  500.9 11.7 %cholesky.181 = f32[128,128]{1,0:T(8,128)S(1)} custom-call(f32[128,128]{1,0:T(8,128)S(1)} %convolution_subtract_fusion.3), custom_call_target="Cholesky" | custom-call | tf_op jit(solution)/shard_map/jit(cholesky)/cholesky | solution.py:26
  512.7 0.7 compare_reduce_fusion
  513.4 0.6 compare_reduce_fusion.1
  516.1 6.0 while.1
  516.1 0.1 constant_dynamic-slice_fusion.2
  516.2 0.5 fusion.37
  516.7 1.4 bitcast_dynamic-update-slice_fusion.2
  518.1 0.1 constant_dynamic-slice_fusion.2
  518.2 0.5 fusion.37
  518.7 1.4 bitcast_dynamic-update-slice_fusion.2
  520.1 0.1 constant_dynamic-slice_fusion.2
  520.2 0.5 fusion.37
  520.7 1.4 bitcast_dynamic-update-slice_fusion.2
  522.1 0.0 copy-start.12
  522.1 29.5 %custom-call.25 = f32[3,128,128]{1,2,0:T(8,128)S(1)} custom-call(f32[3,128,128]{2,1,0:T(8,128)S(1)} %get-tuple-element.11), custom_call_target="InvertDiagBlocksLowerTriangular" | custom-call | tf_op jit(solution)/shard_map/jit(_solve_triangular)/triangular_solve | solution.py:27
  551.6 0.6 fusion.9
  552.3 1.0 convolution_subtract_fusion.1
  553.3 0.6 fusion.17
  553.9 2.9 convolution_subtract_fusion
  556.8 0.6 fusion.15
  557.5 30.4 %fusion = f32[2048,384]{1,0:T(8,128)} fusion(f32[1024,2048]{1,0:T(8,128)} %param.4, bf16[1024,2048]{1,0:T(8,128)(2,1)S(1)} %copy-done.2, f32[128,1024]{1,0:T(8,128)S(1)} %fusion.15, f32[128,1024]{1,0:T(8,128)S(1)} %fusion.17, f32[128,1024]{1,0:T(8,128)S(1)} %fusion.9), kind=kOutput, calls=%fused_computation.6 | convolution fusion | flops 9670754304 | bytes 17301504 | tf_op jit(solution)/shard_map/dot_general | solution.py:29
  587.8 0.0 all-reduce.9.cloned.1.call-update
  587.9 0.0 all-gather.2.cloned.1.call-start
  588.0 1.3 fusion.5
  589.3 0.0 all-gather.2.cloned.1.call-update
  589.3 126.5 %all-reduce.9.cloned.1.call-done = f32[2048,384]{1,0:T(8,128)} async-done(((f32[2048,384]{1,0:T(8,128)}), f32[2048,384]{1,0:T(8,128)}) %all-reduce.9.cloned.1.call-update) | async-done | bytes 3145744 | tf_op jit(solution)/shard_map/psum | solution.py:30
  715.8 2.3 multiply_reduce_fusion
  718.1 6.2 psum.39
  724.4 0.0 copy-start.10
  724.4 1.9 broadcast_divide_fusion
  726.3 1.7 copy-done.3
  728.0 0.2 copy-done.6
  728.1 0.2 copy-done.8
  728.4 0.2 copy-done.10
  728.6 23.8 %multiply_subtract_fusion = f32[1024,2048]{1,0:T(8,128)} fusion(f32[2048,384]{1,0:T(8,128)S(1)} %copy-done.4, f32[1024,2048]{1,0:T(8,128)} %param.4, bf16[1024,2048]{1,0:T(8,128)(2,1)S(1)} %copy-done.3, f32[128,1024]{1,0:T(8,128)S(1)} %copy-done.10, f32[128,1024]{1,0:T(8,128)S(1)} %copy-done.8, f32[128,1024]{1,0:T(8,128)S(1)} %copy-done.6), kind=kOutput, calls=%fused_computation.3 | convolution fusion | flops 9674948608 | bytes 25690112 | tf_op jit(solution)/shard_map/dot_general | solution.py:33
  752.3 79.8 %all-gather.2.cloned.1.call-done = f32[4096,384]{0,1:T(8,128)} async-done(((f32[1024,384]{0,1:T(8,128)}), f32[4096,384]{0,1:T(8,128)}) %all-gather.2.cloned.1.call-update) | async-done | bytes 6291472 | tf_op jit(solution)/shard_map/all_gather | solution.py:28
  832.2 83.8 %multiply_convert_fusion = bf16[4096,2048]{1,0:T(8,128)(2,1)} fusion(f32[4096,384]{0,1:T(8,128)} %all-gather.2.cloned.1.call-done, f32[2048,384]{1,0:T(8,128)} %broadcast_divide_fusion), kind=kOutput, calls=%fused_computation.2 | convolution fusion | flops 38671482880 | bytes 26214400 | tf_op jit(solution)/shard_map/dot_general | solution.py:35
  (30 shorter events, 0.3 us)
Async XLA Ops:
  7.2 286.4 %copy-start = (f32[2048,384]{1,0:T(8,128)S(1)}, f32[2048,384]{1,0:T(8,128)}, u32[]{:S(2)}) copy-start(f32[2048,384]{1,0:T(8,128)} %param.5) | copy-start | bytes 9437188
  7.2 286.4 %reduce-scatter.2.cloned.1.call-start = ((), (), s32[]{:S(2)}) async-start(), calls=%async_computation.1 | async-start | bytes 20971520 | tf_op jit(solution)/shard_map/reduce_scatter | solution.py:16
  7.9 347.0 %all-reduce.5.cloned.1.call-start = ((), (), s32[]{:S(2)}) async-start(), calls=%async_computation.2 | async-start | bytes 3145728 | tf_op jit(solution)/shard_map/psum | solution.py:21
  311.3 142.6 %all-reduce.7.cloned.1.call-start = ((), (), s32[]{:S(2)}) async-start(), calls=%async_computation.3 | async-start | bytes 1179648 | tf_op jit(solution)/shard_map/psum | solution.py:25
  378.5 5.8 copy-start.11
  384.0 331.7 %all-reduce.9.cloned.1.call-start = ((), (), s32[]{:S(2)}) async-start(), calls=%async_computation.5 | async-start | bytes 6291456 | tf_op jit(solution)/shard_map/psum | solution.py:30
  522.1 30.2 %copy-start.12 = (f32[384,384]{1,0:T(8,128)}, f32[384,384]{1,0:T(8,128)S(1)}, u32[]{:S(2)}) copy-start(f32[384,384]{1,0:T(8,128)S(1)} %get-tuple-element.96) | copy-start | bytes 1769476
  552.3 35.7 %copy-start.5 = (f32[128,1024]{1,0:T(8,128)}, f32[128,1024]{1,0:T(8,128)S(1)}, u32[]{:S(2)}) copy-start(f32[128,1024]{1,0:T(8,128)S(1)} %fusion.9) | copy-start | bytes 1572868
  552.3 5.2 copy-start.2
  553.9 34.0 %copy-start.7 = (f32[128,1024]{1,0:T(8,128)}, f32[128,1024]{1,0:T(8,128)S(1)}, u32[]{:S(2)}) copy-start(f32[128,1024]{1,0:T(8,128)S(1)} %fusion.17) | copy-start | bytes 1572868
  557.5 30.5 %copy-start.9 = (f32[128,1024]{1,0:T(8,128)}, f32[128,1024]{1,0:T(8,128)S(1)}, u32[]{:S(2)}) copy-start(f32[128,1024]{1,0:T(8,128)S(1)} %fusion.15) | copy-start | bytes 1572868
  587.9 244.3 %all-gather.2.cloned.1.call-start = ((), (), s32[]{:S(2)}) async-start(), calls=%async_computation.4 | async-start | bytes 7864320 | tf_op jit(solution)/shard_map/all_gather | solution.py:28
  715.8 8.6 copy-start.4
  724.3 3.6 copy-start.3
  724.4 3.8 copy-start.6
  724.4 4.0 copy-start.8
  724.4 4.2 copy-start.10
  832.2 83.8 %copy-start.1 = (f32[2048,384]{1,0:T(8,128)S(1)}, f32[2048,384]{1,0:T(8,128)}, u32[]{:S(2)}) copy-start(f32[2048,384]{1,0:T(8,128)} %param.5) | copy-start | bytes 9437188
Sparse Core Ops, SparseCore 0:
  10.3 283.1 reduce-scatter.1
  311.4 43.4 all-reduce.4
  384.2 69.6 all-reduce.6
  588.0 127.7 all-reduce.8
  717.8 114.3 all-gather.1
where the time goes:
time: 930 us; the launch traced here: 923 us
  waiting for transfers between devices  606 us (65%)
  matrix products  168 us (18%)
  other arithmetic  95.1 us (10%)
  blocking collectives  27.6 us (3%)
  between operations  16.3 us (2%)
  local copies, waits for them, and re-layouts  9.64 us (1%)
    reduce_scatter x1, waiting for transfers between devices, local(): lax.psum_scatter(local_grad.astype(jnp.bfloat16), 'rep', scatter_dimensio...  286 us
    psum x1, waiting for transfers between devices, local(): back = lax.psum(back, ('rep', 'row'))  126 us
    dot_general x1, matrix products, local(): jnp.dot(tile_orth, new_basis.T, precision=HIGH)  83.8 us
    all_gather x1, waiting for transfers between devices, local(): tile_orth = lax.all_gather(orth, 'rep', axis=0, tiled=True)  79.8 us
    psum x1, waiting for transfers between devices, local(): gram = lax.psum(jnp.dot(scaled.T, scaled, precision=HIGH), ('rep', 'row'))  69.4 us
    another operation x10, other arithmetic, local(): factor = jnp.linalg.cholesky(gram)  56.6 us
    psum x1, waiting for transfers between devices, local(): power = lax.psum(power, 'col')  43.6 us
    dot_general x1, matrix products, local(): back = jnp.dot(blended.T, orth, precision=HIGH)  30.4 us
  transfers between devices with their start and end apart: 5, of which 5 were waited for; matrix products, arithmetic and copies ran while one was open for 3% of the time, Pallas kernels for 0%

commit v1 on v0

--- a/solution.py
+++ b/solution.py
@@ -27,7 +27,7 @@
     orth = jax.scipy.linalg.solve_triangular(factor, scaled.T, lower=True).T
     tile_orth = lax.all_gather(orth, "rep", axis=0, tiled=True)
     back = jnp.dot(blended.T, orth, precision=HIGH)
-    back = lax.psum(back, ("rep", "row"))
+    back = lax.psum(lax.psum(back, "row"), "rep")
     back_squares = lax.psum(jnp.sum(back * back, axis=0), "col")
     new_basis = back / (jnp.sqrt(back_squares) + EPS)
     new_momentum = blended - FEEDBACK * jnp.dot(orth, back.T, precision=HIGH)

time: 930 us -> 1010 us (1.086)
  waiting for transfers between devices: 606 us -> 686 us
    psum x1 -> x2, waiting for transfers between devices: 126 us -> 207 us  [local(): back = lax.psum(lax.psum(back, 'row'), 'rep')]
  transfers between devices with their start and end apart: 5 -> 6, of which waited for: 5 -> 6; matrix products, arithmetic and copies ran while one was open for 3% -> 3% of each run, Pallas kernels for 0% -> 0%
where the time goes in v1:
time: 1010 us; the launch traced here: 1000 us
  waiting for transfers between devices  686 us (68%)
  matrix products  168 us (17%)
  other arithmetic  95.1 us (9%)
  blocking collectives  27.8 us (3%)
  between operations  16.6 us (2%)
    reduce_scatter x1, waiting for transfers between devices, local(): lax.psum_scatter(local_grad.astype(jnp.bfloat16), 'rep', scatter_dimensio...  286 us
    psum x2, waiting for transfers between devices, local(): back = lax.psum(lax.psum(back, 'row'), 'rep')  207 us
    dot_general x1, matrix products, local(): jnp.dot(tile_orth, new_basis.T, precision=HIGH)  83.8 us
    all_gather x1, waiting for transfers between devices, local(): tile_orth = lax.all_gather(orth, 'rep', axis=0, tiled=True)  79.6 us
    psum x1, waiting for transfers between devices, local(): gram = lax.psum(jnp.dot(scaled.T, scaled, precision=HIGH), ('rep', 'row'))  69.4 us
    another operation x10, other arithmetic, local(): factor = jnp.linalg.cholesky(gram)  56.6 us
    psum x1, waiting for transfers between devices, local(): power = lax.psum(power, 'col')  43.6 us
    dot_general x1, matrix products, local(): back = jnp.dot(blended.T, orth, precision=HIGH)  30.4 us
  transfers between devices with their start and end apart: 6, of which 6 were waited for; matrix products, arithmetic and copies ran while one was open for 3% of the time, Pallas kernels for 0%

profile of v1, /device:TPU:0, one launch (start us, length us, event | category | flops | bytes accessed | tf_op | source)
XLA Modules:
  0.0 1003.3 jit_solution(17673271234168836671)
XLA Ops:
  7.2 0.0 reduce-scatter.2.cloned.1.call-start
  7.2 0.7 reduce-scatter.2.cloned.1.call-update
  7.9 0.0 all-reduce.6.cloned.1.call-start
  8.0 285.6 %reduce-scatter.2.cloned.1.call-done = bf16[1024,2048]{1,0:T(8,128)(2,1)} async-done(((bf16[4096,2048]{1,0:T(8,128)(2,1)}), bf16[1024,2048]{1,0:T(8,128)(2,1)}) %reduce-scatter.2.cloned.1.call-update) | async-done | bytes 4194320 | tf_op jit(solution)/shard_map/reduce_scatter | solution.py:16
  293.5 17.7 %fusion.1 = f32[1024,384]{1,0:T(8,128)} fusion(f32[2048,384]{1,0:T(8,128)S(1)} %copy-done, f32[1024,2048]{1,0:T(8,128)} %param.4, bf16[1024,2048]{1,0:T(8,128)(2,1)} %reduce-scatter.2.cloned.1.call-done), kind=kOutput, calls=%fused_computation.7 | convolution fusion | flops 9669967872 | bytes 17301504 | tf_op jit(solution)/shard_map/dot_general | solution.py:20
  311.3 0.0 all-reduce.6.cloned.1.call-update
  311.3 0.0 all-reduce.8.cloned.1.call-start
  311.3 43.6 %all-reduce.6.cloned.1.call-done = f32[1024,384]{1,0:T(8,128)} async-done(((f32[1024,384]{1,0:T(8,128)}), f32[1024,384]{1,0:T(8,128)}) %all-reduce.6.cloned.1.call-update) | async-done | bytes 1572880 | tf_op jit(solution)/shard_map/psum | solution.py:21
  354.9 1.6 multiply_reduce_fusion.1
  356.5 21.4 %psum.43 = f32[384]{0:T(512)S(1)} all-reduce(f32[384]{0:T(512)S(1)} %multiply_reduce_fusion.1), channel_id=1, replica_groups=mesh['rep'=4,'row'=2,'col'=4] {'rep','row'}, use_global_device_ids=true, to_apply=%region_3.0 | all-reduce | flops 384 | bytes 3072 | tf_op jit(solution)/shard_map/psum | solution.py:22
  377.9 0.6 multiply_sqrt_fusion
  378.5 5.6 fusion.7
  384.0 0.0 all-reduce.8.cloned.1.call-update
  384.0 0.2 all-reduce.10.cloned.1.call-start
  384.3 0.1 fusion.6
  384.4 69.4 %all-reduce.8.cloned.1.call-done = f32[384,384]{0,1:T(8,128)} async-done(((f32[384,384]{0,1:T(8,128)}), f32[384,384]{0,1:T(8,128)}) %all-reduce.8.cloned.1.call-update) | async-done | bytes 589840 | tf_op jit(solution)/shard_map/psum | solution.py:25
  453.9 1.3 copy.8
  455.1 1.1 fusion.8
  456.3 11.7 %cholesky.77 = f32[128,128]{1,0:T(8,128)S(1)} custom-call(f32[128,128]{1,0:T(8,128)S(1)} %cholesky.192), custom_call_target="Cholesky" | custom-call | tf_op jit(solution)/shard_map/jit(cholesky)/cholesky | solution.py:26
  468.0 9.8 custom-call.23
  477.9 0.3 constant_dynamic-update-slice_fusion.2
  478.2 0.3 convolution_subtract_fusion.2
  478.5 11.7 %cholesky.162 = f32[128,128]{1,0:T(8,128)S(1)} custom-call(f32[128,128]{1,0:T(8,128)S(1)} %cholesky.196), custom_call_target="Cholesky" | custom-call | tf_op jit(solution)/shard_map/jit(cholesky)/cholesky | solution.py:26
  490.2 10.2 %custom-call.24 = f32[1,128,128]{1,2,0:T(8,128)S(1)} custom-call(f32[1,128,128]{2,1,0:T(8,128)S(1)} %get-tuple-element.25), custom_call_target="InvertDiagBlocksLowerTriangular" | custom-call | tf_op jit(solution)/shard_map/jit(cholesky)/cholesky | solution.py:26
  500.4 0.2 convolution_dynamic-update-slice_fusion
  500.6 0.3 convolution_subtract_fusion.3
  500.9 11.7 %cholesky.181 = f32[128,128]{1,0:T(8,128)S(1)} custom-call(f32[128,128]{1,0:T(8,128)S(1)} %convolution_subtract_fusion.3), custom_call_target="Cholesky" | custom-call | tf_op jit(solution)/shard_map/jit(cholesky)/cholesky | solution.py:26
  512.7 0.7 compare_reduce_fusion
  513.4 0.6 compare_reduce_fusion.1
  516.1 6.0 while.1
  516.1 0.1 constant_dynamic-slice_fusion.2
  516.2 0.5 fusion.37
  516.7 1.4 bitcast_dynamic-update-slice_fusion.2
  518.1 0.1 constant_dynamic-slice_fusion.2
  518.2 0.5 fusion.37
  518.7 1.4 bitcast_dynamic-update-slice_fusion.2
  520.1 0.1 constant_dynamic-slice_fusion.2
  520.2 0.5 fusion.37
  520.7 1.4 bitcast_dynamic-update-slice_fusion.2
  522.1 29.5 %custom-call.25 = f32[3,128,128]{1,2,0:T(8,128)S(1)} custom-call(f32[3,128,128]{2,1,0:T(8,128)S(1)} %get-tuple-element.11), custom_call_target="InvertDiagBlocksLowerTriangular" | custom-call | tf_op jit(solution)/shard_map/jit(_solve_triangular)/triangular_solve | solution.py:27
  551.6 0.6 fusion.9
  552.3 1.0 convolution_subtract_fusion.1
  553.3 0.6 fusion.17
  553.9 2.9 convolution_subtract_fusion
  556.8 0.6 fusion.15
  557.5 30.4 %fusion = f32[2048,384]{1,0:T(8,128)} fusion(f32[1024,2048]{1,0:T(8,128)} %param.4, bf16[1024,2048]{1,0:T(8,128)(2,1)S(1)} %copy-done.2, f32[128,1024]{1,0:T(8,128)S(1)} %fusion.15, f32[128,1024]{1,0:T(8,128)S(1)} %fusion.17, f32[128,1024]{1,0:T(8,128)S(1)} %fusion.9), kind=kOutput, calls=%fused_computation.6 | convolution fusion | flops 9670754304 | bytes 17301504 | tf_op jit(solution)/shard_map/dot_general | solution.py:29
  587.8 0.0 all-reduce.10.cloned.1.call-update
  587.9 0.0 all-reduce.12.cloned.1.call-start
  587.9 84.9 %all-reduce.10.cloned.1.call-done = f32[2048,384]{1,0:T(8,128)} async-done(((f32[2048,384]{1,0:T(8,128)}), f32[2048,384]{1,0:T(8,128)}) %all-reduce.10.cloned.1.call-update) | async-done | bytes 3145744 | tf_op jit(solution)/shard_map/psum | solution.py:30
  672.8 0.0 all-reduce.12.cloned.1.call-update
  672.8 0.0 all-gather.2.cloned.1.call-start
  672.9 1.3 fusion.5
  674.2 0.0 all-gather.2.cloned.1.call-update
  674.2 121.9 %all-reduce.12.cloned.1.call-done = f32[2048,384]{1,0:T(8,128)} async-done(((f32[2048,384]{1,0:T(8,128)}), f32[2048,384]{1,0:T(8,128)}) %all-reduce.12.cloned.1.call-update) | async-done | bytes 3145744 | tf_op jit(solution)/shard_map/psum | solution.py:30
  796.1 2.3 multiply_reduce_fusion
  798.5 6.4 psum.47
  804.9 1.9 broadcast_divide_fusion
  806.8 1.8 copy-done.3
  808.5 0.2 copy-done.6
  808.7 0.2 copy-done.8
  808.9 0.2 copy-done.10
  809.1 23.7 %multiply_subtract_fusion = f32[1024,2048]{1,0:T(8,128)} fusion(f32[2048,384]{1,0:T(8,128)S(1)} %copy-done.4, f32[1024,2048]{1,0:T(8,128)} %param.4, bf16[1024,2048]{1,0:T(8,128)(2,1)S(1)} %copy-done.3, f32[128,1024]{1,0:T(8,128)S(1)} %copy-done.10, f32[128,1024]{1,0:T(8,128)S(1)} %copy-done.8, f32[128,1024]{1,0:T(8,128)S(1)} %copy-done.6), kind=kOutput, calls=%fused_computation.3 | convolution fusion | flops 9674948608 | bytes 25690112 | tf_op jit(solution)/shard_map/dot_general | solution.py:33
  832.9 79.6 %all-gather.2.cloned.1.call-done = f32[4096,384]{0,1:T(8,128)} async-done(((f32[1024,384]{0,1:T(8,128)}), f32[4096,384]{0,1:T(8,128)}) %all-gather.2.cloned.1.call-update) | async-done | bytes 6291472 | tf_op jit(solution)/shard_map/all_gather | solution.py:28
  912.5 83.8 %multiply_convert_fusion = bf16[4096,2048]{1,0:T(8,128)(2,1)} fusion(f32[4096,384]{0,1:T(8,128)} %all-gather.2.cloned.1.call-done, f32[2048,384]{1,0:T(8,128)} %broadcast_divide_fusion), kind=kOutput, calls=%fused_computation.2 | convolution fusion | flops 38671482880 | bytes 26214400 | tf_op jit(solution)/shard_map/dot_general | solution.py:35
  (33 shorter events, 0.3 us)
Async XLA Ops:
  7.2 286.4 %copy-start = (f32[2048,384]{1,0:T(8,128)S(1)}, f32[2048,384]{1,0:T(8,128)}, u32[]{:S(2)}) copy-start(f32[2048,384]{1,0:T(8,128)} %param.5) | copy-start | bytes 9437188
  7.2 286.4 %reduce-scatter.2.cloned.1.call-start = ((), (), s32[]{:S(2)}) async-start(), calls=%async_computation.1 | async-start | bytes 20971520 | tf_op jit(solution)/shard_map/reduce_scatter | solution.py:16
  7.9 347.0 %all-reduce.6.cloned.1.call-start = ((), (), s32[]{:S(2)}) async-start(), calls=%async_computation.2 | async-start | bytes 3145728 | tf_op jit(solution)/shard_map/psum | solution.py:21
  311.3 142.6 %all-reduce.8.cloned.1.call-start = ((), (), s32[]{:S(2)}) async-start(), calls=%async_computation.3 | async-start | bytes 1179648 | tf_op jit(solution)/shard_map/psum | solution.py:25
  378.5 5.8 copy-start.11
  384.0 288.8 %all-reduce.10.cloned.1.call-start = ((), (), s32[]{:S(2)}) async-start(), calls=%async_computation.5 | async-start | bytes 6291456 | tf_op jit(solution)/shard_map/psum | solution.py:30
  522.1 30.2 %copy-start.12 = (f32[384,384]{1,0:T(8,128)}, f32[384,384]{1,0:T(8,128)S(1)}, u32[]{:S(2)}) copy-start(f32[384,384]{1,0:T(8,128)S(1)} %get-tuple-element.100) | copy-start | bytes 1769476
  552.3 120.6 %copy-start.5 = (f32[128,1024]{1,0:T(8,128)}, f32[128,1024]{1,0:T(8,128)S(1)}, u32[]{:S(2)}) copy-start(f32[128,1024]{1,0:T(8,128)S(1)} %fusion.9) | copy-start | bytes 1572868
  552.3 5.2 copy-start.2
  553.9 119.0 %copy-start.7 = (f32[128,1024]{1,0:T(8,128)}, f32[128,1024]{1,0:T(8,128)S(1)}, u32[]{:S(2)}) copy-start(f32[128,1024]{1,0:T(8,128)S(1)} %fusion.17) | copy-start | bytes 1572868
  557.5 115.4 %copy-start.9 = (f32[128,1024]{1,0:T(8,128)}, f32[128,1024]{1,0:T(8,128)S(1)}, u32[]{:S(2)}) copy-start(f32[128,1024]{1,0:T(8,128)S(1)} %fusion.15) | copy-start | bytes 1572868
  587.9 208.2 %all-reduce.12.cloned.1.call-start = ((), (), s32[]{:S(2)}) async-start(), calls=%async_computation.6 | async-start | bytes 6291456 | tf_op jit(solution)/shard_map/psum | solution.py:30
  672.8 239.6 %all-gather.2.cloned.1.call-start = ((), (), s32[]{:S(2)}) async-start(), calls=%async_computation.4 | async-start | bytes 7864320 | tf_op jit(solution)/shard_map/all_gather | solution.py:28
  796.1 8.8 copy-start.4
  804.9 3.7 copy-start.3
  804.9 3.8 copy-start.6
  804.9 4.0 copy-start.8
  804.9 4.2 copy-start.10
  912.5 83.8 %copy-start.1 = (f32[2048,384]{1,0:T(8,128)S(1)}, f32[2048,384]{1,0:T(8,128)}, u32[]{:S(2)}) copy-start(f32[2048,384]{1,0:T(8,128)} %param.5) | copy-start | bytes 9437188
Sparse Core Ops, SparseCore 0:
  10.3 283.1 reduce-scatter.1
  311.4 43.4 all-reduce.5
  384.2 69.6 all-reduce.7
  588.0 84.7 all-reduce.9
  675.0 121.0 all-reduce.11
  798.1 114.3 all-gather.1
